TPU v7x, 32 devices: a whole 2x2x4 slice. The times are simulated.
32 devices in a mesh: wide: 16 (over z, x, core), narrow: 2 (over y).
Axes of the slice: x: 2, y: 2, z: 4, core: 2. Of those that a mesh axis runs over, the one named last changes fastest.
Arguments:
- vectors: float32 [1024, 16384], P('narrow', 'wide'), may hold values from -6 to 6
- weights: bfloat16 [5, 64, 256, 512], P(None, 'wide', 'narrow'), may hold values from -0.25 to 0.25
Outputs:
- transformed: float32 [1024, 16384], P('narrow', 'wide')
All inputs are finite; a program needn't handle non-finite values.
Results may differ from a plain program's by a relative error of at most 0.0003.
Values may be sent and summed in bfloat16 or wider, within the bound.
A program may use at most 64 MiB of HBM per device.

v0:
```python
import jax
import jax.numpy as jnp
from jax import lax
from jax.sharding import PartitionSpec as P


def swapped(shard, axis, apart):
    return lax.ppermute(shard, axis, [(i, i ^ 1 << apart) for i in range(lax.axis_size(axis))])


def pair_local(current, level_bit):
    columns, block_count, block_size = current.shape
    stride = 1 << level_bit
    grouped = current.reshape(columns, block_count // (2 * stride), 2, stride, block_size)
    paired = jnp.concatenate([grouped[:, :, 0], grouped[:, :, 1]], -1)
    spread = jnp.broadcast_to(
        paired[:, :, None], (columns, block_count // (2 * stride), 2, stride, 2 * block_size)
    )
    return spread.reshape(columns, block_count, 2 * block_size)


def upper_side(level_bit):
    return lax.axis_index("wide") // (1 << level_bit) % 2


def pair_wide(current, level_bit):
    partner = swapped(current, "wide", level_bit)
    upper_bit = upper_side(level_bit)
    lower_half = jnp.where(upper_bit == 1, partner, current)
    upper_half = jnp.where(upper_bit == 1, current, partner)
    return jnp.concatenate([lower_half, upper_half], -1)


def contract(paired, matrix_rows):
    return jnp.einsum(
        "cbi,boi->cbo", paired, matrix_rows.astype(jnp.float32), precision=lax.Precision.HIGHEST
    )


def gathered_level(paired, level_weight):
    return contract(paired, lax.all_gather(level_weight, "narrow", axis=1, tiled=True))


def on_device(vectors, weights):
    columns, coeffs = vectors.shape
    block_size = weights.shape[3] // 2
    current = vectors.reshape(columns, coeffs // block_size, block_size)
    wide_top = lax.axis_size("wide").bit_length() - 1
    wide_bits = [0, wide_top // 2, wide_top - 1]
    for level_index in range(5):
        if level_index < 2:
            paired = pair_local(current, level_index)
            current = gathered_level(paired, weights[level_index])
        else:
            paired = pair_wide(current, wide_bits[level_index - 2])
            current = gathered_level(paired, weights[level_index])
    return current.reshape(columns, coeffs)


def solution(mesh):
    placed = (P("narrow", "wide"), P(None, "wide", "narrow", None))
    return jax.shard_map(
        on_device, mesh=mesh, in_specs=placed, out_specs=P("narrow", "wide"), check_vma=False
    )
```

profile of v0, /device:TPU:0, one launch (start us, length us, event | category | flops | bytes accessed | tf_op | source)
XLA Modules:
  0.0 252.6 jit_solution(388550160827460083)
XLA Ops:
  6.5 3.2 %fusion.27 = (bf16[1,4,128,512]{3,2,1,0:T(8,128)(2,1)}, bf16[1,4,128,512]{3,2,1,0:T(8,128)(2,1)}, bf16[1,4,128,512]{3,2,1,0:T(8,128)(2,1)}, bf16[1,4,128,512]{3,2,1,0:T(8,128)(2,1)}, bf16[1,4,128,512]{3,2,1,0:T(8,128)(2,1)}) fusion(bf16[5,4,128,512]{3,2,1,0:T(8,128)(2,1)} %param.3), kind=kLoop, calls=%fused_computation.37 | loop fusion | bytes 5242880 | tf_op jit(solution)/shard_map/slice | solution.py:56
  9.8 0.7 all-gather.13.cloned.1.call-update
  10.6 3.0 %reshape_reshape.3 = f32[512,2,2,1,256]{4,2,1,0,3:T(2,128)S(1)} reshape(f32[512,1024]{1,0:T(8,128)} %param.2) | data formatting | bytes 4194304 | tf_op jit(solution)/shard_map/reshape;reshape | solution.py:14
  13.6 1.1 slice_bitcast_fusion.2
  14.7 0.7 slice_bitcast_fusion.3
  15.4 1.8 pad_maximum_fusion
  17.2 0.4 copy.15
  17.7 16.3 %all-gather.11.cloned.1.call-done = bf16[1,4,256,512]{3,2,1,0:T(8,128)(2,1)} async-done(((bf16[1,4,128,512]{3,2,1,0:T(8,128)(2,1)}), bf16[1,4,256,512]{3,2,1,0:T(8,128)(2,1)}) %all-gather.11.cloned.1.call-update) | async-done | bytes 1048592 | tf_op jit(solution)/shard_map/all_gather | solution.py:41
  33.9 0.6 broadcast_in_dim.21
  34.6 0.6 copy-done.1
  35.2 2.3 fusion.22
  37.4 0.2 slice_bitcast_fusion.1
  37.6 1.5 maximum_bitcast_fusion
  39.1 1.9 copy.5
  41.0 15.7 %all-gather.13.cloned.1.call-done = bf16[1,4,256,512]{3,2,1,0:T(8,128)(2,1)} async-done(((bf16[1,4,128,512]{3,2,1,0:T(8,128)(2,1)}), bf16[1,4,256,512]{3,2,1,0:T(8,128)(2,1)}) %all-gather.13.cloned.1.call-update) | async-done | bytes 1048592 | tf_op jit(solution)/shard_map/all_gather | solution.py:41
  56.8 0.6 broadcast_in_dim.24
  57.4 0.6 copy-done
  58.0 2.3 convolution_bitcast_fusion
  60.4 0.2 all-gather.17.cloned.1.call-start
  60.7 4.0 %collective-permute-done = f32[512,4,256]{0,2,1:T(8,128)} collective-permute-done((f32[512,4,256]{0,2,1:T(8,128)S(1)}, f32[512,4,256]{0,2,1:T(8,128)}, u32[]{:S(2)}, u32[]{:S(2)}) %collective-permute-start) | collective-permute-done | bytes 2097184 | tf_op jit(solution)/shard_map/ppermute | solution.py:8
  64.7 4.4 %broadcast_select_fusion.1 = (f32[512,4,256]{0,2,1:T(8,128)}, f32[512,4,256]{0,2,1:T(8,128)}) fusion(f32[512,4,256]{0,2,1:T(8,128)} %collective-permute-done, f32[512,4,256]{0,2,1:T(8,128)S(1)} %convolution_bitcast_fusion, pred[]{:T(512)S(6)} %eq.18), kind=kLoop, calls=%fused_computation.29 | loop fusion | flops 1048576 | bytes 8388609 | tf_op jit(solution)/shard_map/jit(_where)/select_n | solution.py:29
  69.0 13.0 %all-gather.15.cloned.1.call-done = bf16[1,4,256,512]{3,2,1,0:T(8,128)(2,1)} async-done(((bf16[1,4,128,512]{3,2,1,0:T(8,128)(2,1)}), bf16[1,4,256,512]{3,2,1,0:T(8,128)(2,1)}) %all-gather.15.cloned.1.call-update) | async-done | bytes 1048592 | tf_op jit(solution)/shard_map/all_gather | solution.py:41
  82.0 4.6 %fusion.15 = f32[512,4,256]{0,2,1:T(8,128)S(1)} fusion(f32[512,4,256]{0,2,1:T(8,128)} %get-tuple-element.10, f32[512,4,256]{0,2,1:T(8,128)} %get-tuple-element.9, bf16[1,4,256,512]{3,2,1,0:T(8,128)(2,1)} %all-gather.15.cloned.1.call-done), kind=kOutput, calls=%fused_computation.16 | convolution fusion | flops 3222274048 | bytes 7340032 | tf_op jit(solution)/shard_map/cbi,boi->cbo/dot_general | solution.py:35
  86.6 1.6 collective-permute-start.1
  88.3 45.7 %collective-permute-done.1 = f32[512,4,256]{0,2,1:T(8,128)} collective-permute-done((f32[512,4,256]{0,2,1:T(8,128)S(1)}, f32[512,4,256]{0,2,1:T(8,128)}, u32[]{:S(2)}, u32[]{:S(2)}) %collective-permute-start.1) | collective-permute-done | bytes 2097184 | tf_op jit(solution)/shard_map/ppermute | solution.py:8
  134.0 4.4 %broadcast_select_fusion.3 = (f32[512,4,256]{0,2,1:T(8,128)}, f32[512,4,256]{0,2,1:T(8,128)}) fusion(f32[512,4,256]{0,2,1:T(8,128)} %collective-permute-done.1, f32[512,4,256]{0,2,1:T(8,128)S(1)} %fusion.15, pred[]{:T(512)S(6)} %eq.17), kind=kLoop, calls=%fused_computation.31 | loop fusion | flops 1048576 | bytes 8388609 | tf_op jit(solution)/shard_map/jit(_where)/select_n | solution.py:29
  138.3 4.6 %fusion.12 = f32[512,4,256]{0,2,1:T(8,128)S(1)} fusion(f32[512,4,256]{0,2,1:T(8,128)} %get-tuple-element.8, f32[512,4,256]{0,2,1:T(8,128)} %get-tuple-element.7, bf16[1,4,256,512]{3,2,1,0:T(8,128)(2,1)} %all-gather.17.cloned.1.call-done), kind=kOutput, calls=%fused_computation.15 | convolution fusion | flops 3222274048 | bytes 7340032 | tf_op jit(solution)/shard_map/cbi,boi->cbo/dot_general | solution.py:35
  143.0 2.5 collective-permute-start.2
  145.5 89.8 %collective-permute-done.2 = f32[512,4,256]{0,2,1:T(8,128)} collective-permute-done((f32[512,4,256]{0,2,1:T(8,128)S(1)}, f32[512,4,256]{0,2,1:T(8,128)}, u32[]{:S(2)}, u32[]{:S(2)}) %collective-permute-start.2) | collective-permute-done | bytes 2097184 | tf_op jit(solution)/shard_map/ppermute | solution.py:8
  235.3 4.4 %broadcast_select_fusion.5 = (f32[512,4,256]{0,2,1:T(8,128)}, f32[512,4,256]{0,2,1:T(8,128)}) fusion(f32[512,4,256]{0,2,1:T(8,128)} %collective-permute-done.2, f32[512,4,256]{0,2,1:T(8,128)S(1)} %fusion.12, pred[]{:T(512)S(6)} %eq.16), kind=kLoop, calls=%fused_computation.33 | loop fusion | flops 1048576 | bytes 8388609 | tf_op jit(solution)/shard_map/jit(_where)/select_n | solution.py:29
  239.7 4.6 %fusion.8 = f32[4,512,256]{1,2,0:T(8,128)S(1)} fusion(f32[512,4,256]{0,2,1:T(8,128)} %get-tuple-element.6, f32[512,4,256]{0,2,1:T(8,128)} %get-tuple-element.5, bf16[1,4,256,512]{3,2,1,0:T(8,128)(2,1)} %all-gather.19.cloned.1.call-done), kind=kOutput, calls=%fused_computation.8 | convolution fusion | flops 3222274048 | bytes 7340032 | tf_op jit(solution)/shard_map/cbi,boi->cbo/dot_general | solution.py:35
  244.3 1.8 copy.9
  (13 shorter events, 0.3 us)
Async XLA Ops:
  6.5 27.4 %all-gather.11.cloned.1.call-start = ((), (), s32[]{:S(2)}) async-start(), calls=%async_computation | async-start | bytes 1572864 | tf_op jit(solution)/shard_map/all_gather | solution.py:41
  9.8 47.0 %all-gather.13.cloned.1.call-start = ((), (), s32[]{:S(2)}) async-start(), calls=%async_computation.1 | async-start | bytes 1572864 | tf_op jit(solution)/shard_map/all_gather | solution.py:41
  10.5 71.5 %all-gather.15.cloned.1.call-start = ((), (), s32[]{:S(2)}) async-start(), calls=%async_computation.2 | async-start | bytes 1572864 | tf_op jit(solution)/shard_map/all_gather | solution.py:41
  33.9 1.2 copy-start.1
  56.8 1.2 copy-start
  60.3 4.4 %collective-permute-start = (f32[512,4,256]{0,2,1:T(8,128)S(1)}, f32[512,4,256]{0,2,1:T(8,128)}, u32[]{:S(2)}, u32[]{:S(2)}) collective-permute-start(f32[512,4,256]{0,2,1:T(8,128)S(1)} %convolution_bitcast_fusion), channel_id=1, source_target_pairs={{0,2},{2,0},{4,6},{6,4},{8,10},{10,8},{12,14},{14,12},{16,18},{18,... | collective-permute-start | bytes 6291464 | tf_op jit(solution)/shard_map/ppermute | solution.py:8
  60.4 77.9 %all-gather.17.cloned.1.call-start = ((), (), s32[]{:S(2)}) async-start(), calls=%async_computation.3 | async-start | bytes 1572864 | tf_op jit(solution)/shard_map/all_gather | solution.py:41
  86.6 47.4 %collective-permute-start.1 = (f32[512,4,256]{0,2,1:T(8,128)S(1)}, f32[512,4,256]{0,2,1:T(8,128)}, u32[]{:S(2)}, u32[]{:S(2)}) collective-permute-start(f32[512,4,256]{0,2,1:T(8,128)S(1)} %fusion.15), channel_id=1, source_target_pairs={{0,8},{2,10},{4,12},{6,14},{8,0},{10,2},{12,4},{14,6},{16,24},{18,... | collective-permute-start | bytes 6291464 | tf_op jit(solution)/shard_map/ppermute | solution.py:8
  88.2 151.5 %all-gather.19.cloned.1.call-start = ((), (), s32[]{:S(2)}) async-start(), calls=%async_computation.4 | async-start | bytes 1572864 | tf_op jit(solution)/shard_map/all_gather | solution.py:41
  143.0 92.4 %collective-permute-start.2 = (f32[512,4,256]{0,2,1:T(8,128)S(1)}, f32[512,4,256]{0,2,1:T(8,128)}, u32[]{:S(2)}, u32[]{:S(2)}) collective-permute-start(f32[512,4,256]{0,2,1:T(8,128)S(1)} %fusion.12), channel_id=1, source_target_pairs={{0,16},{2,18},{4,20},{6,22},{8,24},{10,26},{12,28},{14,30},{16,0},... | collective-permute-start | bytes 6291464 | tf_op jit(solution)/shard_map/ppermute | solution.py:8
Sparse Core Ops, SparseCore 0:
  9.9 23.9 all-gather.10
  35.5 21.2 all-gather.12
  60.5 21.4 all-gather.14
  88.3 20.3 all-gather.16
  145.6 19.4 all-gather.18
where the time goes:
time: 253 us
  waiting for transfers between devices  185 us (73%)
  matrix products  18.4 us (7%)
  other arithmetic  16.3 us (6%)
  local copies, waits for them, and re-layouts  14.8 us (6%)
  between operations  13.3 us (5%)
  starting transfers between devices  4.44 us (2%)
    ppermute x3, waiting for transfers between devices, swapped(): lax.ppermute(shard, axis, [(i, i ^ 1 << apart) for i in range(lax.axis_si...  140 us
    all_gather x5, waiting for transfers between devices, gathered_level(): lax.all_gather(level_weight, 'narrow', axis=1, tiled=True)  45 us
    dot_general x5, matrix products, contract(): jnp.einsum('cbi,boi->cbo', paired, matrix_rows.astype(jnp.float32), preci...  18.4 us
    select_n x3, other arithmetic, pair_wide(): lower_half = jnp.where(upper_bit == 1, partner, current)  13.1 us
  transfers between devices with their start and end apart: 8, of which 6 were waited for; matrix products, arithmetic and copies ran while one was open for 11% of the time, Pallas kernels for 0%

commit v1 on v0

v1 whole, which is shorter than its diff:
```python
import functools

import jax
import jax.numpy as jnp
from jax import lax
from jax.experimental import pallas as pl
from jax.experimental.pallas import tpu as pltpu
from jax.sharding import PartitionSpec as P

MESH = pl.DeviceIdType.MESH
POWER = 12
TOP = 2.0 ** (126 / POWER)
TINY = 1e-35
TILE = 256
WINDOW = 5
BF16 = jnp.bfloat16
F32 = jnp.float32

WEIGHT_ORDER = (
    (0, 0), (0, 2), (1, 0), (2, 0), (1, 2), (2, 2), (3, 0), (3, 2),
    (0, 1), (0, 3), (1, 1), (2, 1), (1, 3), (2, 3), (3, 1), (3, 3),
    (4, 0), (4, 2), (4, 1), (4, 3),
)
COMPUTE_ORDER = (
    (0, 0), (0, 2), (1, 0), (1, 2), (2, 0), (2, 2), (3, 0), (0, 1), (3, 2), (0, 3),
    (1, 1), (1, 3), (2, 1), (2, 3), (3, 1), (3, 3),
    (4, 0), (4, 2), (4, 1), (4, 3),
)


def split(value):
    high = value.astype(BF16)
    return high, (value - high.astype(F32)).astype(BF16)


def encode(value):
    scale = jnp.maximum(jnp.max(jnp.abs(value), axis=0, keepdims=True), TINY)
    t = value * (TOP / scale)
    t2 = t * t
    t4 = t2 * t2
    t12 = t4 * t4 * t4
    return jnp.where(t < 0, -t12, t12).astype(BF16), scale


def decode(code, scale):
    wide = code.astype(F32)
    size = jnp.exp(jnp.log(jnp.abs(wide)) * (1.0 / POWER)) * (scale * (1.0 / TOP))
    return jnp.where(wide == 0, 0.0, jnp.where(wide < 0, -size, size))


def kernel(
    peers, strides, x_hbm, w_hbm, out_hbm,
    x, w, l0, l1, l1_in, l2, z1_out, z1_in, s1_out, s1_in, l3, z2_out, z2_in, s2_out, s2_in, out,
    x_sem, own_sem, w_send, w_recv, core_send, core_recv, z_send, z_recv, s_send, s_recv, out_sem,
):
    columns = x.shape[0]
    size = w.shape[3] // 2
    rows = w_hbm.shape[2]
    blocks = w.shape[1]
    tiles = columns // TILE
    me_n = lax.axis_index("narrow")
    me_w = lax.axis_index("wide")
    sides = [me_w // stride % 2 for stride in strides]
    partners = [me_w + (1 - 2 * side) * stride for side, stride in zip(sides, strides)]

    def x_copy(half):
        span = pl.ds(half * 2 * size, 2 * size)
        return pltpu.make_async_copy(x_hbm.at[:, span], x.at[:, span], x_sem.at[half])

    def own_copy(level, block):
        span = pl.ds(pl.multiple_of(me_n * rows, rows), rows)
        return pltpu.make_async_copy(
            w_hbm.at[level, block], w.at[level, block, span], own_sem.at[level, block]
        )

    def weight_copy(level, block, k, owner):
        span = pl.ds(pl.multiple_of(owner * rows, rows), rows)
        return pltpu.make_async_remote_copy(
            src_ref=w_hbm.at[level, block],
            dst_ref=w.at[level, block, span],
            send_sem=w_send.at[level, block, k - 1],
            recv_sem=w_recv.at[level, block, k - 1],
            device_id={"narrow": lax.rem(me_n + k, peers)},
            device_id_type=MESH,
        )

    def send_weight(position):
        if position < len(WEIGHT_ORDER):
            level, block = WEIGHT_ORDER[position]
            for k in range(1, peers):
                weight_copy(level, block, k, me_n).start()

    def core_copy(block):
        return pltpu.make_async_remote_copy(
            src_ref=l1.at[block], dst_ref=l1_in.at[block],
            send_sem=core_send.at[block], recv_sem=core_recv.at[block],
            device_id={"wide": partners[0]}, device_id_type=MESH,
        )

    def code_copies(level, block):
        source, target = ((z1_out, z1_in), (z2_out, z2_in))[level]
        s_source, s_target = ((s1_out, s1_in), (s2_out, s2_in))[level]
        partner = partners[level + 1]
        return (
            pltpu.make_async_remote_copy(
                src_ref=s_source.at[block], dst_ref=s_target.at[block],
                send_sem=s_send.at[level, block], recv_sem=s_recv.at[level, block],
                device_id={"wide": partner}, device_id_type=MESH,
            ),
            pltpu.make_async_remote_copy(
                src_ref=source.at[block], dst_ref=target.at[block],
                send_sem=z_send.at[level, block], recv_sem=z_recv.at[level, block],
                device_id={"wide": partner}, device_id_type=MESH,
            ),
        )

    def out_copy(block):
        return pltpu.make_async_copy(
            out.at[block], out_hbm.at[:, pl.ds(block * size, size)], out_sem.at[block]
        )

    def product(level, block, first, second, side, finish):
        def step(tile, carry):
            total = None
            for part, half in ((first, side), (second, 1 - side)):
                start = half * size
                if not isinstance(half, int):
                    start = pl.multiple_of(start, size)
                matrix = w[level, block, :, pl.ds(start, size)]
                lhs = jnp.concatenate(part(tile), axis=0)
                term = lax.dot_general(
                    lhs, matrix, (((1,), (1,)), ((), ())), preferred_element_type=F32
                )
                total = term if total is None else total + term
            finish(tile, total[:TILE] + total[TILE:])
            return carry

        lax.fori_loop(0, tiles, step, 0)

    def at_tile(tile):
        return pl.ds(pl.multiple_of(tile * TILE, TILE), TILE)

    def at_scale(tile):
        return pl.ds(pl.multiple_of(tile * 8, 8), 8)

    def from_x(block):
        return lambda tile: split(x[at_tile(tile), pl.ds(block * size, size)])

    def from_pair(ref, block):
        return lambda tile: (ref[block, 0, at_tile(tile)], ref[block, 1, at_tile(tile)])

    def from_code(ref, scales, block):
        return lambda tile: split(
            decode(ref[block, at_tile(tile)], scales[block, at_scale(tile)][:1])
        )

    def to_pair(ref, block):
        def finish(tile, value):
            high, low = split(value)
            ref[block, 0, at_tile(tile)] = high
            ref[block, 1, at_tile(tile)] = low

        return finish

    def to_code(ref, code_ref, scale_ref, block):
        keep = to_pair(ref, block)

        def finish(tile, value):
            keep(tile, value)
            code, scale = encode(value)
            code_ref[block, at_tile(tile)] = code
            scale_ref[block, at_scale(tile)] = jnp.broadcast_to(scale, (8, size))

        return finish

    def to_out(block):
        def finish(tile, value):
            out[block, at_tile(tile)] = value

        return finish

    for half in range(blocks // 2):
        x_copy(half).start()
    for level, block in WEIGHT_ORDER:
        own_copy(level, block).start()

    barrier = pltpu.get_barrier_semaphore()
    for k in range(1, peers):
        pl.semaphore_signal(
            barrier, inc=1, device_id={"narrow": lax.rem(me_n + k, peers)}, device_id_type=MESH
        )
    for partner in partners:
        pl.semaphore_signal(barrier, inc=1, device_id={"wide": partner}, device_id_type=MESH)
    pl.semaphore_wait(barrier, peers - 1 + len(partners))

    for position in range(WINDOW):
        send_weight(position)

    arrived = [0]

    def need_weight(level, block):
        while (level, block) in WEIGHT_ORDER[arrived[0]:]:
            next_level, next_block = WEIGHT_ORDER[arrived[0]]
            own_copy(next_level, next_block).wait()
            for k in range(1, peers):
                weight_copy(
                    next_level, next_block, k, lax.rem(me_n + peers - k, peers)
                ).wait_recv()
            send_weight(arrived[0] + WINDOW)
            arrived[0] += 1

    x_ready = set()
    for level, block in COMPUTE_ORDER:
        if level == 0 and block // 2 not in x_ready:
            x_copy(block // 2).wait()
            x_ready.add(block // 2)
        need_weight(level, block)
        if level < 2:
            stride = 1 << level
            low = block - block // stride % 2 * stride
            high = low + stride
        if level == 0:
            product(level, block, from_x(low), from_x(high), 0, to_pair(l0, block))
        elif level == 1:
            product(level, block, from_pair(l0, low), from_pair(l0, high), 0, to_pair(l1, block))
            core_copy(block).start()
        elif level == 2:
            core_copy(block).wait_recv()
            product(
                level, block, from_pair(l1, block), from_pair(l1_in, block), sides[0],
                to_code(l2, z1_out, s1_out, block),
            )
            for copy in code_copies(0, block):
                copy.start()
        elif level == 3:
            for copy in code_copies(0, block):
                copy.wait_recv()
            product(
                level, block, from_pair(l2, block), from_code(z1_in, s1_in, block), sides[1],
                to_code(l3, z2_out, s2_out, block),
            )
            for copy in code_copies(1, block):
                copy.start()
        else:
            for copy in code_copies(1, block):
                copy.wait_recv()
            product(
                level, block, from_pair(l3, block), from_code(z2_in, s2_in, block), sides[2],
                to_out(block),
            )
            out_copy(block).start()

    for level, block in WEIGHT_ORDER:
        for k in range(1, peers):
            weight_copy(level, block, k, me_n).wait_send()
    for block in range(blocks):
        core_copy(block).wait_send()
        for level in range(2):
            for copy in code_copies(level, block):
                copy.wait_send()
        out_copy(block).wait()


def on_device(vectors, weights):
    columns, coeffs = vectors.shape
    levels, blocks, rows, depth = weights.shape
    size = depth // 2
    peers = lax.axis_size("narrow")
    wide_top = lax.axis_size("wide").bit_length() - 1
    strides = [1 << bit for bit in (0, wide_top // 2, wide_top - 1)]
    tiles = columns // TILE
    pair = pltpu.VMEM((blocks, 2, columns, size), BF16)
    code = pltpu.VMEM((blocks, columns, size), BF16)
    scale = pltpu.VMEM((blocks, tiles * 8, size), F32)
    dma = pltpu.SemaphoreType.DMA
    return pl.pallas_call(
        functools.partial(kernel, peers, strides),
        out_shape=jax.ShapeDtypeStruct((columns, coeffs), F32),
        in_specs=[pl.BlockSpec(memory_space=pl.ANY)] * 2,
        out_specs=pl.BlockSpec(memory_space=pl.ANY),
        scratch_shapes=[
            pltpu.VMEM((columns, coeffs), F32),
            pltpu.VMEM((levels, blocks, size, depth), BF16),
            pair, pair, pair, pair,
            code, code, scale, scale,
            pair,
            code, code, scale, scale,
            pltpu.VMEM((blocks, columns, size), F32),
            dma((blocks // 2,)),
            dma((levels, blocks)),
            dma((levels, blocks, max(peers - 1, 1))),
            dma((levels, blocks, max(peers - 1, 1))),
            dma((blocks,)),
            dma((blocks,)),
            dma((2, blocks)),
            dma((2, blocks)),
            dma((2, blocks)),
            dma((2, blocks)),
            dma((blocks,)),
        ],
        compiler_params=pltpu.CompilerParams(
            collective_id=0, has_side_effects=True, vmem_limit_bytes=60 * 1024 * 1024
        ),
    )(vectors, weights)


def solution(mesh):
    placed = (P("narrow", "wide"), P(None, "wide", "narrow", None))
    return jax.shard_map(
        on_device, mesh=mesh, in_specs=placed, out_specs=P("narrow", "wide"), check_vma=False
    )
```

time: 253 us -> 89.6 us (0.35)
  waiting for transfers between devices: 185 us -> 0 us
  Pallas kernels: 0 us -> 85.1 us
  matrix products: 18.4 us -> 0 us
  other arithmetic: 16.3 us -> 0 us
  between operations: 13.3 us -> 0.01 us
  local copies, waits for them, and re-layouts: 14.8 us -> 3.16 us
  starting transfers between devices: 4.44 us -> 0 us
    ppermute x3 -> x0, waiting for transfers between devices: 140 us -> none  [swapped(): lax.ppermute(shard, axis, [(i, i ^ 1 << apart) for i in range(lax.axis_si...]
    pallas_call x0 -> x1, Pallas kernels: none -> 85.1 us  [on_device(): pl.pallas_call(functools.partial(kernel, peers, strides), out_shape=jax.S...]
    all_gather x5 -> x0, waiting for transfers between devices: 45 us -> none  [gathered_level(): lax.all_gather(level_weight, 'narrow', axis=1, tiled=True)]
    dot_general x5 -> x0, matrix products: 18.4 us -> none  [contract(): jnp.einsum('cbi,boi->cbo', paired, matrix_rows.astype(jnp.float32), preci...]
    select_n x3 -> x0, other arithmetic: 13.1 us -> none  [pair_wide(): lower_half = jnp.where(upper_bit == 1, partner, current)]
    ppermute x3 -> x0, starting transfers between devices: 4.1 us -> none  [swapped(): lax.ppermute(shard, axis, [(i, i ^ 1 << apart) for i in range(lax.axis_si...]
    broadcast_in_dim x4 -> x0, local copies, waits for them, and re-layouts: 3.5 us -> none  [pair_local(): jnp.broadcast_to(paired[:, :, None], (columns, block_count // (2 * stride...]
    slice x1 -> x0, local copies, waits for them, and re-layouts: 3.21 us -> none  [on_device(): current = gathered_level(paired, weights[level_index])]
  transfers between devices with their start and end apart: 8 -> 0, of which waited for: 6 -> 0; matrix products, arithmetic and copies ran while one was open for 11% -> 0% of each run, Pallas kernels for 0% -> 0%
where the time goes in v1:
time: 89.6 us; the launch traced here: 88.2 us
  Pallas kernels  85.1 us (95%)
  local copies, waits for them, and re-layouts  3.16 us (4%)
    pallas_call x1, Pallas kernels, on_device(): pl.pallas_call(functools.partial(kernel, peers, strides), out_shape=jax.S...  85.1 us
    unnamed x1, local copies, waits for them, and re-layouts  3.16 us

profile of v1, /device:TPU:0, one launch (start us, length us, event | category | flops | bytes accessed | tf_op | source)
XLA Modules:
  0.0 88.2 jit_solution(203733794502989680)
XLA Ops:
  0.0 85.1 %shard_map.28 = f32[512,1024]{1,0:T(8,128)} custom-call(f32[512,1024]{1,0:T(8,128)} %x_hbm.1, bf16[5,4,128,512]{3,2,1,0:T(8,128)(2,1)} %w_hbm.1), custom_call_target="tpu_custom_call" | custom-call | tf_op jit(solution)/shard_map/pallas_call | solution.py:276
  85.1 3.2 %copy.4 = f32[512,1024]{1,0:T(8,128)} copy(f32[512,1024]{1,0:T(8,128)} %shard_map.28) | data formatting | bytes 4194304

commit v2 on v1

--- a/solution.py
+++ b/solution.py
@@ -17,13 +17,13 @@
 F32 = jnp.float32
 
 WEIGHT_ORDER = (
-    (0, 0), (0, 2), (1, 0), (2, 0), (1, 2), (2, 2), (3, 0), (3, 2),
-    (0, 1), (0, 3), (1, 1), (2, 1), (1, 3), (2, 3), (3, 1), (3, 3),
+    (0, 0), (0, 2), (1, 0), (2, 0), (1, 2), (2, 2), (3, 0), (0, 1),
+    (0, 3), (1, 1), (2, 1), (3, 2), (1, 3), (2, 3), (3, 1), (3, 3),
     (4, 0), (4, 2), (4, 1), (4, 3),
 )
 COMPUTE_ORDER = (
-    (0, 0), (0, 2), (1, 0), (1, 2), (2, 0), (2, 2), (3, 0), (0, 1), (3, 2), (0, 3),
-    (1, 1), (1, 3), (2, 1), (2, 3), (3, 1), (3, 3),
+    (0, 0), (0, 2), (1, 0), (1, 2), (2, 0), (2, 2), (3, 0), (0, 1), (0, 3),
+    (1, 1), (2, 1), (3, 2), (1, 3), (2, 3), (3, 1), (3, 3),
     (4, 0), (4, 2), (4, 1), (4, 3),
 )
 
@@ -49,9 +49,9 @@
 
 
 def kernel(
-    peers, strides, x_hbm, w_hbm, out_hbm,
-    x, w, l0, l1, l1_in, l2, z1_out, z1_in, s1_out, s1_in, l3, z2_out, z2_in, s2_out, s2_in, out,
-    x_sem, own_sem, w_send, w_recv, core_send, core_recv, z_send, z_recv, s_send, s_recv, out_sem,
+    peers, strides, x_hbm, w_hbm, out,
+    x, w, l0, l1, l1_in, l2, z1_out, z1_in, s1_out, s1_in, l3, z2_out, z2_in, s2_out, s2_in,
+    x_sem, own_sem, w_send, w_recv, core_send, core_recv, z_send, z_recv, s_send, s_recv,
 ):
     columns = x.shape[0]
     size = w.shape[3] // 2
@@ -97,26 +97,21 @@
             device_id={"wide": partners[0]}, device_id_type=MESH,
         )
 
-    def code_copies(level, block):
+    def code_copies(level, block, tile):
         source, target = ((z1_out, z1_in), (z2_out, z2_in))[level]
         s_source, s_target = ((s1_out, s1_in), (s2_out, s2_in))[level]
         partner = partners[level + 1]
         return (
             pltpu.make_async_remote_copy(
-                src_ref=s_source.at[block], dst_ref=s_target.at[block],
-                send_sem=s_send.at[level, block], recv_sem=s_recv.at[level, block],
+                src_ref=s_source.at[block, tile], dst_ref=s_target.at[block, tile],
+                send_sem=s_send.at[level, block, tile], recv_sem=s_recv.at[level, block, tile],
                 device_id={"wide": partner}, device_id_type=MESH,
             ),
             pltpu.make_async_remote_copy(
-                src_ref=source.at[block], dst_ref=target.at[block],
-                send_sem=z_send.at[level, block], recv_sem=z_recv.at[level, block],
+                src_ref=source.at[block, at_tile(tile)], dst_ref=target.at[block, at_tile(tile)],
+                send_sem=z_send.at[level, block, tile], recv_sem=z_recv.at[level, block, tile],
                 device_id={"wide": partner}, device_id_type=MESH,
             ),
-        )
-
-    def out_copy(block):
-        return pltpu.make_async_copy(
-            out.at[block], out_hbm.at[:, pl.ds(block * size, size)], out_sem.at[block]
         )
 
     def product(level, block, first, second, side, finish):
@@ -140,19 +135,21 @@
     def at_tile(tile):
         return pl.ds(pl.multiple_of(tile * TILE, TILE), TILE)
 
-    def at_scale(tile):
-        return pl.ds(pl.multiple_of(tile * 8, 8), 8)
-
     def from_x(block):
         return lambda tile: split(x[at_tile(tile), pl.ds(block * size, size)])
 
     def from_pair(ref, block):
         return lambda tile: (ref[block, 0, at_tile(tile)], ref[block, 1, at_tile(tile)])
 
-    def from_code(ref, scales, block):
-        return lambda tile: split(
-            decode(ref[block, at_tile(tile)], scales[block, at_scale(tile)][:1])
-        )
+    def from_code(level, block):
+        ref, scales = ((z1_in, s1_in), (z2_in, s2_in))[level]
+
+        def load(tile):
+            for copy in code_copies(level, block, tile):
+                copy.wait_recv()
+            return split(decode(ref[block, at_tile(tile)], scales[block, tile]))
+
+        return load
 
     def to_pair(ref, block):
         def finish(tile, value):
@@ -162,20 +159,23 @@
 
         return finish
 
-    def to_code(ref, code_ref, scale_ref, block):
-        keep = to_pair(ref, block)
+    def to_code(level, block):
+        keep = to_pair((l2, l3)[level], block)
+        code_ref, scale_ref = ((z1_out, s1_out), (z2_out, s2_out))[level]
 
         def finish(tile, value):
             keep(tile, value)
             code, scale = encode(value)
             code_ref[block, at_tile(tile)] = code
-            scale_ref[block, at_scale(tile)] = jnp.broadcast_to(scale, (8, size))
+            scale_ref[block, tile] = scale
+            for copy in code_copies(level, block, tile):
+                copy.start()
 
         return finish
 
     def to_out(block):
         def finish(tile, value):
-            out[block, at_tile(tile)] = value
+            out[at_tile(tile), pl.ds(block * size, size)] = value
 
         return finish
 
@@ -228,27 +228,17 @@
             core_copy(block).wait_recv()
             product(
                 level, block, from_pair(l1, block), from_pair(l1_in, block), sides[0],
-                to_code(l2, z1_out, s1_out, block),
+                to_code(0, block),
             )
-            for copy in code_copies(0, block):
-                copy.start()
         elif level == 3:
-            for copy in code_copies(0, block):
-                copy.wait_recv()
             product(
-                level, block, from_pair(l2, block), from_code(z1_in, s1_in, block), sides[1],
-                to_code(l3, z2_out, s2_out, block),
+                level, block, from_pair(l2, block), from_code(0, block), sides[1],
+                to_code(1, block),
             )
-            for copy in code_copies(1, block):
-                copy.start()
         else:
-            for copy in code_copies(1, block):
-                copy.wait_recv()
             product(
-                level, block, from_pair(l3, block), from_code(z2_in, s2_in, block), sides[2],
-                to_out(block),
+                level, block, from_pair(l3, block), from_code(1, block), sides[2], to_out(block)
             )
-            out_copy(block).start()
 
     for level, block in WEIGHT_ORDER:
         for k in range(1, peers):
@@ -256,9 +246,9 @@
     for block in range(blocks):
         core_copy(block).wait_send()
         for level in range(2):
-            for copy in code_copies(level, block):
-                copy.wait_send()
-        out_copy(block).wait()
+            for tile in range(tiles):
+                for copy in code_copies(level, block, tile):
+                    copy.wait_send()
 
 
 def on_device(vectors, weights):
@@ -271,13 +261,13 @@
     tiles = columns // TILE
     pair = pltpu.VMEM((blocks, 2, columns, size), BF16)
     code = pltpu.VMEM((blocks, columns, size), BF16)
-    scale = pltpu.VMEM((blocks, tiles * 8, size), F32)
+    scale = pltpu.VMEM((blocks, tiles, 1, size), F32)
     dma = pltpu.SemaphoreType.DMA
     return pl.pallas_call(
         functools.partial(kernel, peers, strides),
-        out_shape=jax.ShapeDtypeStruct((columns, coeffs), F32),
-        in_specs=[pl.BlockSpec(memory_space=pl.ANY)] * 2,
-        out_specs=pl.BlockSpec(memory_space=pl.ANY),
+        out_shape=pltpu.VMEM((columns, coeffs), F32),
+        in_specs=[pl.BlockSpec(memory_space=pltpu.HBM)] * 2,
+        out_specs=pl.BlockSpec(memory_space=pltpu.VMEM),
         scratch_shapes=[
             pltpu.VMEM((columns, coeffs), F32),
             pltpu.VMEM((levels, blocks, size, depth), BF16),
@@ -285,21 +275,19 @@
             code, code, scale, scale,
             pair,
             code, code, scale, scale,
-            pltpu.VMEM((blocks, columns, size), F32),
             dma((blocks // 2,)),
             dma((levels, blocks)),
             dma((levels, blocks, max(peers - 1, 1))),
             dma((levels, blocks, max(peers - 1, 1))),
             dma((blocks,)),
             dma((blocks,)),
-            dma((2, blocks)),
-            dma((2, blocks)),
-            dma((2, blocks)),
-            dma((2, blocks)),
-            dma((blocks,)),
+            dma((2, blocks, tiles)),
+            dma((2, blocks, tiles)),
+            dma((2, blocks, tiles)),
+            dma((2, blocks, tiles)),
         ],
         compiler_params=pltpu.CompilerParams(
-            collective_id=0, has_side_effects=True, vmem_limit_bytes=60 * 1024 * 1024
+            collective_id=0, has_side_effects=True, vmem_limit_bytes=40 * 1024 * 1024
         ),
     )(vectors, weights)
 

time: 89.6 us -> 86.1 us (0.961); the launches traced: 88.2 us -> 85.9 us
  Pallas kernels: 85.1 us -> 81.2 us
  local copies, waits for them, and re-layouts: 3.16 us -> 4.65 us
    pallas_call x1, Pallas kernels: 85.1 us -> 81.2 us  [on_device(): pl.pallas_call(functools.partial(kernel, peers, strides), out_shape=pltpu...]
    unnamed x1 -> x5, local copies, waits for them, and re-layouts: 3.16 us -> 4.65 us
where the time goes in v2:
time: 86.1 us; the launch traced here: 85.9 us
  Pallas kernels  81.2 us (94%)
  local copies, waits for them, and re-layouts  4.65 us (5%)
    pallas_call x1, Pallas kernels, on_device(): pl.pallas_call(functools.partial(kernel, peers, strides), out_shape=pltpu...  81.2 us
    unnamed x5, local copies, waits for them, and re-layouts  4.65 us

profile of v2, /device:TPU:0, one launch (start us, length us, event | category | flops | bytes accessed | tf_op | source)
XLA Modules:
  0.0 85.9 jit_solution(13520266980982360820)
XLA Ops:
  0.0 0.0 copy-start
  0.0 1.7 %copy-done = bf16[5,4,128,512]{3,2,1,0:T(8,128)(2,1)S(1)} copy-done((bf16[5,4,128,512]{3,2,1,0:T(8,128)(2,1)S(1)}, bf16[5,4,128,512]{3,2,1,0:T(8,128)(2,1)}, u32[]{:S(2)}) %copy-start) | copy-done | bytes 2621464
  1.7 0.0 copy-start.1
  1.7 1.6 %copy-done.1 = f32[512,1024]{1,0:T(8,128)S(1)} copy-done((f32[512,1024]{1,0:T(8,128)S(1)}, f32[512,1024]{1,0:T(8,128)}, u32[]{:S(2)}) %copy-start.1) | copy-done | bytes 2097176
  3.3 81.2 %shard_map.28 = f32[512,1024]{1,0:T(8,128)S(1)} custom-call(f32[512,1024]{1,0:T(8,128)S(1)} %copy-done.1, bf16[5,4,128,512]{3,2,1,0:T(8,128)(2,1)S(1)} %copy-done), custom_call_target="tpu_custom_call" | custom-call | tf_op jit(solution)/shard_map/pallas_call | solution.py:266
  84.6 1.3 %copy.4 = f32[512,1024]{1,0:T(8,128)} copy(f32[512,1024]{1,0:T(8,128)S(1)} %shard_map.28) | data formatting | bytes 4194304
Async XLA Ops:
  0.0 1.7 %copy-start = (bf16[5,4,128,512]{3,2,1,0:T(8,128)(2,1)S(1)}, bf16[5,4,128,512]{3,2,1,0:T(8,128)(2,1)}, u32[]{:S(2)}) copy-start(bf16[5,4,128,512]{3,2,1,0:T(8,128)(2,1)} %w_hbm.1) | copy-start | bytes 7864324
  1.7 1.6 %copy-start.1 = (f32[512,1024]{1,0:T(8,128)S(1)}, f32[512,1024]{1,0:T(8,128)}, u32[]{:S(2)}) copy-start(f32[512,1024]{1,0:T(8,128)} %x_hbm.1) | copy-start | bytes 6291460
